TPU v7x, 32 devices: a whole 2x2x4 slice. The times are simulated.
32 devices in a mesh: samp: 4 (over x, core), snp: 8 (over z, y).
Axes of the slice: x: 2, y: 2, z: 4, core: 2. Of those that a mesh axis runs over, the one named last changes fastest.
Arguments:
- genotypes: float32 [4096, 8192], P('samp', 'snp'), may hold values from -1 to 2, as said below
Outputs:
- band_r: float32 [8192, 4096], P('snp', 'samp')
Inputs may be any that keep to these rules, and one draw needn't show every extreme that they name: `genotypes`: -1 marks a missing dosage; every other value lies between 0 and 2. Every eighth sample (samples 0, 8, 16, ...) has no missing dosage, and over those samples each SNP's dosages run through 0, 1, 2 cyclically from a SNP's own starting value.
All inputs are finite; a program needn't handle non-finite values.
Results may differ from a plain program's by a relative error of at most 0.006.
Values may be sent and summed in bfloat16 or wider, within the bound.
A program may use at most 64 MiB of HBM per device.

v0:
```python
import jax
import jax.numpy as jnp
from jax import lax
from jax.sharding import PartitionSpec as P

TILE = 512
BAND = 4096


EPS = 1e-05


def passed_along(x, axis, by):
    count = lax.axis_size(axis)
    pairs = [(i, i + by) for i in range(count) if 0 <= i + by < count]
    return lax.ppermute(x, axis, pairs)


def on_device(genotypes):
    present = (genotypes >= 0).astype(jnp.float32)
    dosage = genotypes * present
    counted, summed, squared = lax.psum(
        (jnp.sum(present, axis=0), jnp.sum(dosage, axis=0), jnp.sum(dosage * dosage, axis=0)),
        "samp",
    )
    average = summed / counted
    spread = squared / counted - average * average
    scaled = (present * (dosage - average) * lax.rsqrt(spread + EPS)).astype(jnp.bfloat16)
    col_norms = counted * spread / (spread + EPS)
    snp_dev = genotypes.shape[1]
    tiles_dev = snp_dev // TILE
    panels = (BAND - TILE + 2 * snp_dev - 1) // snp_dev - 1
    span_cols = (panels + 1) * snp_dev
    pieces = [scaled]
    norm_pieces = [col_norms]
    current = scaled
    current_norm = col_norms
    for distance in range(1, panels + 1):
        current = passed_along(current, "snp", -1)
        pieces.append(current)
        current_norm = passed_along(current_norm, "snp", -1)
        norm_pieces.append(current_norm)
    extended = jnp.concatenate(pieces, axis=1)
    device_pos = lax.axis_index("snp")
    far_norms = jnp.concatenate(norm_pieces)
    columns = device_pos * snp_dev + jnp.arange(span_cols, dtype=jnp.int32)
    inside = columns < lax.axis_size("snp") * snp_dev
    far_norms = jnp.where(inside, far_norms, 1.0)
    quarter = BAND // lax.axis_size("samp")
    partial_value = []
    for tile_pos in range(tiles_dev):
        row_block = scaled[:, tile_pos * TILE : (tile_pos + 1) * TILE]
        col_block = extended[:, tile_pos * TILE : tile_pos * TILE + BAND]
        partial_value.append(
            lax.dot_general(
                row_block, col_block, (((0,), (0,)), ((), ())), preferred_element_type=jnp.float32
            )
        )
    summed_tiles = jnp.concatenate(partial_value, axis=0)
    shares = lax.psum_scatter(summed_tiles, "samp", scatter_dimension=1, tiled=True)
    samp_pos = lax.axis_index("samp")
    results = []
    for tile_pos in range(tiles_dev):
        col_norm = lax.dynamic_slice_in_dim(
            far_norms, tile_pos * TILE + samp_pos * quarter, quarter, 0
        )
        row_norm = col_norms[tile_pos * TILE : (tile_pos + 1) * TILE]
        block_share = shares[tile_pos * TILE : (tile_pos + 1) * TILE]
        results.append(block_share / jnp.sqrt(row_norm[:, None] * col_norm[None, :]))
    return jnp.concatenate(results, axis=0)


def solution(mesh):
    in_specs = (P("samp", "snp"),)
    out_specs = P("snp", "samp")
    return jax.shard_map(
        on_device, mesh=mesh, in_specs=in_specs, out_specs=out_specs, check_vma=False
    )
```

profile of v0, /device:TPU:15, one launch (start us, length us, event | category | flops | bytes accessed | tf_op | source)
XLA Modules:
  0.0 369.2 jit_solution(1272068576149341026)
XLA Ops:
  6.5 0.0 reduce-scatter.2.cloned.1.call-start
  6.5 3.2 multiply_reduce_fusion
  9.7 9.7 %all-reduce = (f32[1024]{0:T(1024)S(1)}, f32[1024]{0:T(1024)S(1)}, f32[1024]{0:T(1024)S(1)}) all-reduce(f32[1024]{0:T(1024)S(1)} %get-tuple-element.6, f32[1024]{0:T(1024)S(1)} %get-tuple-element.7, f32[1024]{0:T(1024)S(1)} %get-tuple-element.5), channel_id=1, replica_groups=mesh['samp'=4,'snp'=8] {'samp'}, use_global_device_ids=true, to_apply=%region_1.0 | all-reduce | flops 3072 | bytes 24576 | tf_op jit(solution)/shard_map/psum | solution.py:22
  19.4 3.1 constant_dynamic-update-slice_fusion.4
  22.6 2.1 collective-permute-start
  24.7 46.7 %collective-permute-done = bf16[1024,1024]{1,0:T(8,128)(2,1)S(1)} collective-permute-done((bf16[1024,1024]{1,0:T(8,128)(2,1)S(1)}, bf16[1024,1024]{1,0:T(8,128)(2,1)S(1)}, u32[]{:S(2)}, u32[]{:S(2)}) %collective-permute-start) | collective-permute-done | bytes 2097184 | tf_op jit(solution)/shard_map/ppermute | solution.py:16
  71.4 1.9 collective-permute-start.1
  73.3 46.0 %collective-permute-done.1 = bf16[1024,1024]{1,0:T(8,128)(2,1)S(1)} collective-permute-done((bf16[1024,1024]{1,0:T(8,128)(2,1)S(1)}, bf16[1024,1024]{1,0:T(8,128)(2,1)S(1)}, u32[]{:S(2)}, u32[]{:S(2)}) %collective-permute-start.1) | collective-permute-done | bytes 2097184 | tf_op jit(solution)/shard_map/ppermute | solution.py:16
  119.4 1.9 collective-permute-start.2
  121.3 45.3 %collective-permute-done.2 = bf16[1024,1024]{1,0:T(8,128)(2,1)} collective-permute-done((bf16[1024,1024]{1,0:T(8,128)(2,1)S(1)}, bf16[1024,1024]{1,0:T(8,128)(2,1)}, u32[]{:S(2)}, u32[]{:S(2)}) %collective-permute-start.2) | collective-permute-done | bytes 2097184 | tf_op jit(solution)/shard_map/ppermute | solution.py:16
  166.6 2.1 collective-permute-start.3
  168.7 0.2 constant_dynamic-update-slice_fusion.3
  168.9 0.2 constant_dynamic-update-slice_fusion.2
  169.0 0.0 copy-done
  169.0 1.8 constant_dynamic-update-slice_fusion.1
  170.8 9.2 %fusion.2 = f32[512,4096]{1,0:T(8,128)} fusion(bf16[1024,1024]{1,0:T(8,128)(2,1)} %collective-permute-done.2, bf16[1024,1024]{1,0:T(8,128)(2,1)} %copy-done, bf16[1024,1024]{1,0:T(8,128)(2,1)S(1)} %collective-permute-done, bf16[1024,1024]{1,0:T(8,128)(2,1)S(1)} %get-tuple-element.15), kind=kOutput, calls=%fused_computation.3 | convolution fusion | flops 4328521728 | bytes 17825792 | tf_op jit(solution)/shard_map/dot_general | solution.py:55
  180.0 33.1 %collective-permute-done.3 = bf16[1024,1024]{1,0:T(8,128)(2,1)} collective-permute-done((bf16[1024,1024]{1,0:T(8,128)(2,1)}, bf16[1024,1024]{1,0:T(8,128)(2,1)}, u32[]{:S(2)}, u32[]{:S(2)}) %collective-permute-start.3) | collective-permute-done | bytes 2097184 | tf_op jit(solution)/shard_map/ppermute | solution.py:16
  213.1 1.8 constant_dynamic-update-slice_fusion
  214.9 4.6 %fusion = f32[512,4096]{1,0:T(8,128)S(1)} fusion(bf16[1024,5120]{1,0:T(8,128)(2,1)S(1)} %constant_dynamic-update-slice_fusion, bf16[1024,1024]{1,0:T(8,128)(2,1)S(1)} %get-tuple-element.15), kind=kOutput, calls=%fused_computation.1 | convolution fusion | flops 4294967296 | bytes 17825792 | tf_op jit(solution)/shard_map/dot_general | solution.py:55
  219.5 10.1 %pad_maximum_fusion = f32[1024,4096]{1,0:T(8,128)} fusion(f32[512,4096]{1,0:T(8,128)S(1)} %fusion, f32[512,4096]{1,0:T(8,128)} %fusion.2), kind=kLoop, calls=%fused_computation | loop fusion | flops 4194304 | bytes 33554432 | tf_op jit(solution)/shard_map/concatenate | solution.py:59
  229.7 0.0 reduce-scatter.2.cloned.1.call-update
  229.7 1.9 collective-permute-start.4
  231.6 3.3 collective-permute-done.4
  234.9 1.9 collective-permute-start.5
  236.9 3.4 collective-permute-done.5
  240.3 1.9 collective-permute-start.6
  242.2 3.3 collective-permute-done.6
  245.5 1.9 collective-permute-start.7
  247.4 3.3 collective-permute-done.7
  250.8 0.1 fusion.15
  250.8 106.8 %reduce-scatter.2.cloned.1.call-done = f32[1024,1024]{1,0:T(8,128)} async-done(((f32[1024,4096]{1,0:T(8,128)}), f32[1024,1024]{1,0:T(8,128)}) %reduce-scatter.2.cloned.1.call-update) | async-done | bytes 4194320 | tf_op jit(solution)/shard_map/reduce_scatter | solution.py:60
  357.6 4.8 %slice_multiply_fusion.1 = (f32[1024,1024]{1,0:T(8,128)}, f32[1024,1024]{1,0:T(8,128)}) fusion(f32[1024,1024]{1,0:T(8,128)} %reduce-scatter.2.cloned.1.call-done, f32[1024]{0:T(1024)S(1)} %get-tuple-element.18, f32[512]{0:T(512)S(1)} %get-tuple-element.20, f32[1024]{0:T(1024)S(1)} %get-tuple-element.19, ...), kind=kLoop, output_to_operand_aliasing={{0}: (5, {}), {1}: (5, {})}, calls=%fused_computation.16 | loop fusion | flops 2097152 | bytes 8400896 | tf_op jit(solution)/shard_map/div | solution.py:69
  (10 shorter events, 0.0 us)
Async XLA Ops:
  6.5 351.1 %reduce-scatter.2.cloned.1.call-start = ((), (), s32[]{:S(2)}) async-start(), calls=%async_computation.1 | async-start | bytes 20971520 | tf_op jit(solution)/shard_map/reduce_scatter | solution.py:60
  22.6 48.8 %collective-permute-start = (bf16[1024,1024]{1,0:T(8,128)(2,1)S(1)}, bf16[1024,1024]{1,0:T(8,128)(2,1)S(1)}, u32[]{:S(2)}, u32[]{:S(2)}) collective-permute-start(bf16[1024,1024]{1,0:T(8,128)(2,1)S(1)} %get-tuple-element.15), channel_id=1, source_target_pairs={{1,0},{2,1},{3,2},{4,3},{5,4},{6,5},{7,6},{9,8},{10,9},{11,10},{12... | collective-permute-start | bytes 6291464 | tf_op jit(solution)/shard_map/ppermute | solution.py:16
  71.4 48.0 %collective-permute-start.1 = (bf16[1024,1024]{1,0:T(8,128)(2,1)S(1)}, bf16[1024,1024]{1,0:T(8,128)(2,1)S(1)}, u32[]{:S(2)}, u32[]{:S(2)}) collective-permute-start(bf16[1024,1024]{1,0:T(8,128)(2,1)S(1)} %collective-permute-done), channel_id=1, source_target_pairs={{1,0},{2,1},{3,2},{4,3},{5,4},{6,5},{7,6},{9,8},{10,9},{11,10},{12... | collective-permute-start | bytes 6291464 | tf_op jit(solution)/shard_map/ppermute | solution.py:16
  119.4 49.7 %copy-start = (bf16[1024,1024]{1,0:T(8,128)(2,1)}, bf16[1024,1024]{1,0:T(8,128)(2,1)S(1)}, u32[]{:S(2)}) copy-start(bf16[1024,1024]{1,0:T(8,128)(2,1)S(1)} %collective-permute-done.1) | copy-start | bytes 6291460
  119.4 47.2 %collective-permute-start.2 = (bf16[1024,1024]{1,0:T(8,128)(2,1)S(1)}, bf16[1024,1024]{1,0:T(8,128)(2,1)}, u32[]{:S(2)}, u32[]{:S(2)}) collective-permute-start(bf16[1024,1024]{1,0:T(8,128)(2,1)S(1)} %collective-permute-done.1), channel_id=1, source_target_pairs={{1,0},{2,1},{3,2},{4,3},{5,4},{6,5},{7,6},{9,8},{10,9},{11,10},{12... | collective-permute-start | bytes 6291464 | tf_op jit(solution)/shard_map/ppermute | solution.py:16
  166.6 46.6 %collective-permute-start.3 = (bf16[1024,1024]{1,0:T(8,128)(2,1)}, bf16[1024,1024]{1,0:T(8,128)(2,1)}, u32[]{:S(2)}, u32[]{:S(2)}) collective-permute-start(bf16[1024,1024]{1,0:T(8,128)(2,1)} %collective-permute-done.2), channel_id=1, source_target_pairs={{1,0},{2,1},{3,2},{4,3},{5,4},{6,5},{7,6},{9,8},{10,9},{11,10},{12... | collective-permute-start | bytes 6291464 | tf_op jit(solution)/shard_map/ppermute | solution.py:16
  229.7 5.3 %collective-permute-start.4 = (f32[1024]{0:T(1024)S(1)}, f32[1024]{0:T(1024)S(1)}, u32[]{:S(2)}, u32[]{:S(2)}) collective-permute-start(f32[1024]{0:T(1024)S(1)} %get-tuple-element.12), channel_id=1, source_target_pairs={{1,0},{2,1},{3,2},{4,3},{5,4},{6,5},{7,6},{9,8},{10,9},{11,10},{12... | collective-permute-start | bytes 12296 | tf_op jit(solution)/shard_map/ppermute | solution.py:16
  234.9 5.3 %collective-permute-start.5 = (f32[1024]{0:T(1024)S(1)}, f32[1024]{0:T(1024)S(1)}, u32[]{:S(2)}, u32[]{:S(2)}) collective-permute-start(f32[1024]{0:T(1024)S(1)} %collective-permute-done.4), channel_id=1, source_target_pairs={{1,0},{2,1},{3,2},{4,3},{5,4},{6,5},{7,6},{9,8},{10,9},{11,10},{12... | collective-permute-start | bytes 12296 | tf_op jit(solution)/shard_map/ppermute | solution.py:16
  240.3 5.2 %collective-permute-start.6 = (f32[1024]{0:T(1024)S(1)}, f32[1024]{0:T(1024)S(1)}, u32[]{:S(2)}, u32[]{:S(2)}) collective-permute-start(f32[1024]{0:T(1024)S(1)} %collective-permute-done.5), channel_id=1, source_target_pairs={{1,0},{2,1},{3,2},{4,3},{5,4},{6,5},{7,6},{9,8},{10,9},{11,10},{12... | collective-permute-start | bytes 12296 | tf_op jit(solution)/shard_map/ppermute | solution.py:16
  245.5 5.2 %collective-permute-start.7 = (f32[1024]{0:T(1024)S(1)}, f32[1024]{0:T(1024)S(1)}, u32[]{:S(2)}, u32[]{:S(2)}) collective-permute-start(f32[1024]{0:T(1024)S(1)} %collective-permute-done.6), channel_id=1, source_target_pairs={{1,0},{2,1},{3,2},{4,3},{5,4},{6,5},{7,6},{9,8},{10,9},{11,10},{12... | collective-permute-start | bytes 12296 | tf_op jit(solution)/shard_map/ppermute | solution.py:16
Sparse Core Ops, SparseCore 0:
  229.8 127.7 reduce-scatter.1
where the time goes:
time: 372 us; the launch traced here: 369 us
  waiting for transfers between devices  291 us (78%)
  other arithmetic  21.2 us (6%)
  starting transfers between devices  15.7 us (4%)
  matrix products  13.8 us (4%)
  between operations  13.6 us (4%)
  blocking collectives  9.71 us (3%)
  local copies, waits for them, and re-layouts  3.97 us (1%)
    ppermute x8, waiting for transfers between devices, passed_along(): return lax.ppermute(x, axis, pairs)  184 us
    reduce_scatter x1, waiting for transfers between devices, on_device(): lax.psum_scatter(summed_tiles, 'samp', scatter_dimension=1, tiled=True)  107 us
    ppermute x8, starting transfers between devices, passed_along(): return lax.ppermute(x, axis, pairs)  15.7 us
    dot_general x2, matrix products, on_device(): lax.dot_general(row_block, col_block, (((0,), (0,)), ((), ())), preferred...  13.8 us
    concatenate x1, other arithmetic, on_device(): summed_tiles = jnp.concatenate(partial_value, axis=0)  10.1 us
    psum x1, blocking collectives, on_device(): lax.psum((jnp.sum(present, axis=0), jnp.sum(dosage, axis=0), jnp.sum(dosa...  9.71 us
  transfers between devices with their start and end apart: 9, of which 9 were waited for; matrix products, arithmetic and copies ran while one was open for 3% of the time, Pallas kernels for 0%

commit v1 on v0

v1 whole, which is shorter than its diff:
```python
import jax
import jax.numpy as jnp
from jax import lax
from jax.sharding import PartitionSpec as P

TILE = 512
BAND = 4096
EPS = 1e-05


def exchanged(x, axis, mask):
    count = lax.axis_size(axis)
    return lax.ppermute(x, axis, [(i, i ^ mask) for i in range(count)])


def product(rows, cols):
    return lax.dot_general(
        rows, cols, (((0,), (0,)), ((), ())), preferred_element_type=jnp.float32
    )


def on_device(genotypes):
    present = (genotypes >= 0).astype(jnp.float32)
    dosage = genotypes * present
    stats = jnp.stack(
        [jnp.sum(present, axis=0), jnp.sum(dosage, axis=0), jnp.sum(dosage * dosage, axis=0)]
    )
    stats = stats + exchanged(stats, "samp", 1)
    stats = stats + exchanged(stats, "samp", 2)
    counted, summed, squared = stats[0], stats[1], stats[2]
    average = summed / counted
    spread = squared / counted - average * average
    col_norms = counted * spread / (spread + EPS)
    factor = lax.rsqrt(spread + EPS) * lax.rsqrt(col_norms)
    scaled = (present * (dosage - average) * factor).astype(jnp.bfloat16)

    half = genotypes.shape[1] // 2
    assert half == TILE and BAND == 8 * half
    count = lax.axis_size("snp")
    assert count % 2 == 0 and lax.axis_size("samp") == 4
    odd_down = [(i, i - 1) for i in range(1, count, 2)]
    even_up = [(i, i + 1) for i in range(0, count, 2)]
    two_down = [(i, i - 2) for i in range(2, count)]
    odd_two_down = [(i, i - 2) for i in range(3, count, 2)]
    odd = lax.axis_index("snp") % 2 == 1

    own0, own1 = scaled[:, :half], scaled[:, half:]
    z0 = lax.ppermute(own0, "snp", two_down)
    a0 = lax.ppermute(own0, "snp", odd_down)
    z1 = lax.ppermute(own1, "snp", two_down)
    a1 = lax.ppermute(own1, "snp", odd_down)
    y0 = lax.ppermute(z0, "snp", even_up + odd_down)
    y1 = lax.ppermute(z1, "snp", even_up + odd_down)
    d0 = lax.ppermute(z0, "snp", two_down)
    e0 = lax.ppermute(d0, "snp", even_up)
    e1 = lax.ppermute(y1, "snp", odd_two_down)

    samp = lax.axis_index("samp")
    core = samp % 2
    keep_rows = lax.dynamic_slice_in_dim(scaled, core * half, half, 1)
    send_rows = lax.dynamic_slice_in_dim(scaled, (1 - core) * half, half, 1)

    def chip_sum(cols, pairs):
        given = product(send_rows, cols).astype(jnp.bfloat16)
        got = lax.ppermute(given, "samp", pairs)
        return (product(keep_rows, cols) + got.astype(jnp.float32)).astype(jnp.bfloat16)

    def whole_sum(part, pairs):
        return part + lax.ppermute(part, "samp", pairs)

    swap = [(0, 1), (1, 0), (2, 3), (3, 2)]
    to_low = [(2, 0), (3, 1)]
    to_high = [(0, 2), (1, 3)]
    cat = lambda *xs: jnp.concatenate(xs, axis=1)
    s = [None] * 9
    r01 = chip_sum(scaled, swap)
    w01 = whole_sum(r01, to_low)
    s[0], s[1] = w01[:, :half], w01[:, half:]
    r4 = chip_sum(z0, swap)
    r5 = chip_sum(z1, swap)
    s[4] = whole_sum(r4, [(0, 2), (3, 1)])
    s[5] = whole_sum(r5, to_high)
    s[2] = whole_sum(chip_sum(jnp.where(odd, y0, a0), swap), to_low)
    s[3] = whole_sum(chip_sum(jnp.where(odd, y1, a1), swap), to_low)
    s[8] = whole_sum(chip_sum(d0, [(0, 1), (2, 3)]), [(1, 3)])
    s[6] = whole_sum(chip_sum(jnp.where(odd, e0, y0), swap), to_high)
    s[7] = whole_sum(chip_sum(jnp.where(odd, e1, y1), swap), to_high)

    def chosen(options):
        parts = [cat(s[i], s[j]) for i, j in options]
        return jnp.where(
            samp < 2,
            jnp.where(samp == 0, parts[0], parts[1]),
            jnp.where(samp == 2, parts[2], parts[3]),
        )

    sent = chosen([(2, 3), (1, 2), (6, 7), (5, 6)])
    kept = chosen([(0, 1), (3, 4), (4, 5), (7, 8)])
    got = exchanged(sent, "samp", 1)
    first = jnp.where(core == 0, kept, got)
    second = jnp.where(core == 0, got, kept)
    return jnp.concatenate([first, second], axis=0).astype(jnp.float32)


def solution(mesh):
    return jax.shard_map(
        on_device, mesh=mesh, in_specs=(P("samp", "snp"),), out_specs=P("snp", "samp"),
        check_vma=False,
    )
```

time: 372 us -> 190 us (0.51)
  the two profiles are of different devices: /device:TPU:15 before, /device:TPU:27 now
where the time goes in v1:
time: 190 us; the launch traced here: 189 us
  waiting for transfers between devices  80.3 us (42%)
  starting transfers between devices  50 us (26%)
  matrix products  35.3 us (19%)
  other arithmetic  19.5 us (10%)
  local copies, waits for them, and re-layouts  3.41 us (2%)
    dot_general x16, matrix products, product(): lax.dot_general(rows, cols, (((0,), (0,)), ((), ())), preferred_element_t...  35.3 us
    ppermute x1, waiting for transfers between devices, on_device(): a1 = lax.ppermute(own1, 'snp', odd_down)  19.6 us
    ppermute x1, waiting for transfers between devices, on_device(): z1 = lax.ppermute(own1, 'snp', two_down)  16 us
    ppermute x8, starting transfers between devices, whole_sum(): return part + lax.ppermute(part, 'samp', pairs)  16 us
    ppermute x8, waiting for transfers between devices, whole_sum(): return part + lax.ppermute(part, 'samp', pairs)  15 us
    ppermute x1, waiting for transfers between devices, on_device(): z0 = lax.ppermute(own0, 'snp', two_down)  12.6 us
    ppermute x8, starting transfers between devices, chip_sum(): got = lax.ppermute(given, 'samp', pairs)  12.5 us
    add x8, other arithmetic, whole_sum(): return part + lax.ppermute(part, 'samp', pairs)  9.03 us
  transfers between devices with their start and end apart: 28, of which 11 were waited for; matrix products, arithmetic and copies ran while one was open for 24% of the time, Pallas kernels for 0%

profile of v1, /device:TPU:27, one launch (start us, length us, event | category | flops | bytes accessed | tf_op | source)
XLA Modules:
  0.0 189.0 jit_solution(4324039999018677683)
XLA Ops:
  0.0 3.3 %convert_reduce_fusion = (f32[1024]{0:T(1024)S(1)}, f32[1024]{0:T(1024)S(1)}, f32[1024]{0:T(1024)S(1)}) fusion(f32[1024,1024]{1,0:T(8,128)} %param.1), kind=kLoop, calls=%fused_computation.2 | loop fusion | flops 7336960 | bytes 4206592 | tf_op jit(solution)/shard_map/reduce_sum | solution.py:26
  5.3 2.3 %collective-permute-done.1 = f32[3,1024]{1,0:T(4,128)S(1)} collective-permute-done((f32[3,1024]{1,0:T(4,128)S(1)}, f32[3,1024]{1,0:T(4,128)S(1)}, u32[]{:S(2)}, u32[]{:S(2)}) %collective-permute-start.1) | collective-permute-done | bytes 12320 | tf_op jit(solution)/shard_map/ppermute | solution.py:13
  9.6 3.1 %collective-permute-start.9 = (bf16[1024,512]{1,0:T(8,128)(2,1)}, bf16[1024,512]{1,0:T(8,128)(2,1)}, u32[]{:S(2)}, u32[]{:S(2)}) collective-permute-start(bf16[1024,512]{1,0:T(8,128)(2,1)} %get-tuple-element.12), channel_id=1, source_target_pairs={{2,0},{3,1},{4,2},{5,3},{6,4},{7,5},{10,8},{11,9},{12,10},{13,11},... | collective-permute-start | bytes 3145736 | tf_op jit(solution)/shard_map/ppermute | solution.py:48
  12.7 2.3 %collective-permute-start.4 = (bf16[1024,512]{1,0:T(8,128)(2,1)S(1)}, bf16[1024,512]{1,0:T(8,128)(2,1)}, u32[]{:S(2)}, u32[]{:S(2)}) collective-permute-start(bf16[1024,512]{1,0:T(8,128)(2,1)S(1)} %get-tuple-element.13), channel_id=1, source_target_pairs={{2,0},{3,1},{4,2},{5,3},{6,4},{7,5},{10,8},{11,9},{12,10},{13,11},... | collective-permute-start | bytes 3145736 | tf_op jit(solution)/shard_map/ppermute | solution.py:50
  14.9 2.3 %convolution_convert_fusion = bf16[512,1024]{1,0:T(8,128)(2,1)} fusion(bf16[1024,1024]{1,0:T(8,128)(2,1)S(1)} %multiply_convert_fusion, s32[]{:T(128)S(6)} %select_n.84), kind=kOutput, calls=%fused_computation.8 | convolution fusion | flops 1074266112 | bytes 4194308 | tf_op jit(solution)/shard_map/dot_general | solution.py:17
  20.4 12.6 %collective-permute-done.9 = bf16[1024,512]{1,0:T(8,128)(2,1)} collective-permute-done((bf16[1024,512]{1,0:T(8,128)(2,1)}, bf16[1024,512]{1,0:T(8,128)(2,1)}, u32[]{:S(2)}, u32[]{:S(2)}) %collective-permute-start.9) | collective-permute-done | bytes 1048608 | tf_op jit(solution)/shard_map/ppermute | solution.py:48
  34.2 5.1 %collective-permute-start.17 = (bf16[1024,512]{1,0:T(8,128)(2,1)}, bf16[1024,512]{1,0:T(8,128)(2,1)}, u32[]{:S(2)}, u32[]{:S(2)}) collective-permute-start(bf16[1024,512]{1,0:T(8,128)(2,1)} %collective-permute-done.9), channel_id=1, source_target_pairs={{2,0},{3,1},{4,2},{5,3},{6,4},{7,5},{10,8},{11,9},{12,10},{13,11},... | collective-permute-start | bytes 3145736 | tf_op jit(solution)/shard_map/ppermute | solution.py:54
  39.3 16.0 %collective-permute-done.4 = bf16[1024,512]{1,0:T(8,128)(2,1)} collective-permute-done((bf16[1024,512]{1,0:T(8,128)(2,1)S(1)}, bf16[1024,512]{1,0:T(8,128)(2,1)}, u32[]{:S(2)}, u32[]{:S(2)}) %collective-permute-start.4) | collective-permute-done | bytes 1048608 | tf_op jit(solution)/shard_map/ppermute | solution.py:50
  59.9 4.7 %collective-permute-start.12 = (bf16[512,512]{1,0:T(8,128)(2,1)S(1)}, bf16[512,512]{1,0:T(8,128)(2,1)S(1)}, u32[]{:S(2)}, u32[]{:S(2)}) collective-permute-start(bf16[512,512]{1,0:T(8,128)(2,1)S(1)} %convolution_convert_fusion.5), channel_id=1, source_target_pairs={{0,8},{8,0},{16,24},{24,16},{1,9},{9,1},{17,25},{25,17},{2,10},{10... | collective-permute-start | bytes 1572872 | tf_op jit(solution)/shard_map/ppermute | solution.py:65
  64.5 2.5 %add_convert_fusion = bf16[512,1024]{1,0:T(8,128)(2,1)S(1)} fusion(bf16[512,1024]{1,0:T(8,128)(2,1)} %collective-permute-done.2, bf16[1024,1024]{1,0:T(8,128)(2,1)S(1)} %multiply_convert_fusion, s32[]{:T(128)S(6)} %select_n.83), kind=kOutput, calls=%fused_computation.4 | convolution fusion | flops 1075314688 | bytes 5242884 | tf_op jit(solution)/shard_map/dot_general | solution.py:17
  68.5 2.2 %collective-permute-start.3 = (bf16[512,1024]{1,0:T(8,128)(2,1)S(1)}, bf16[512,1024]{1,0:T(8,128)(2,1)S(1)}, u32[]{:S(2)}, u32[]{:S(2)}) collective-permute-start(bf16[512,1024]{1,0:T(8,128)(2,1)S(1)} %add_convert_fusion), channel_id=1, source_target_pairs={{16,0},{24,8},{17,1},{25,9},{18,2},{26,10},{19,3},{27,11},{20,4},{... | collective-permute-start | bytes 3145736 | tf_op jit(solution)/shard_map/ppermute | solution.py:69
  70.7 7.2 %collective-permute-done.17 = bf16[1024,512]{1,0:T(8,128)(2,1)} collective-permute-done((bf16[1024,512]{1,0:T(8,128)(2,1)}, bf16[1024,512]{1,0:T(8,128)(2,1)}, u32[]{:S(2)}, u32[]{:S(2)}) %collective-permute-start.17) | collective-permute-done | bytes 1048608 | tf_op jit(solution)/shard_map/ppermute | solution.py:54
  77.9 3.2 %collective-permute-start.24 = (bf16[1024,512]{1,0:T(8,128)(2,1)}, bf16[1024,512]{1,0:T(8,128)(2,1)S(1)}, u32[]{:S(2)}, u32[]{:S(2)}) collective-permute-start(bf16[1024,512]{1,0:T(8,128)(2,1)} %collective-permute-done.17), channel_id=1, source_target_pairs={{0,1},{2,3},{4,5},{6,7},{8,9},{10,11},{12,13},{14,15},{16,17},{18,... | collective-permute-start | bytes 3145736 | tf_op jit(solution)/shard_map/ppermute | solution.py:55
  83.2 2.7 %collective-permute-start.22 = (bf16[512,512]{1,0:T(8,128)(2,1)S(1)}, bf16[512,512]{1,0:T(8,128)(2,1)S(1)}, u32[]{:S(2)}, u32[]{:S(2)}) collective-permute-start(bf16[512,512]{1,0:T(8,128)(2,1)S(1)} %convolution_convert_fusion.2), channel_id=1, source_target_pairs={{0,8},{8,0},{16,24},{24,16},{1,9},{9,1},{17,25},{25,17},{2,10},{10... | collective-permute-start | bytes 1572872 | tf_op jit(solution)/shard_map/ppermute | solution.py:65
  85.9 5.1 %collective-permute-done.5 = bf16[1024,512]{1,0:T(8,128)(2,1)} collective-permute-done((bf16[1024,512]{1,0:T(8,128)(2,1)}, bf16[1024,512]{1,0:T(8,128)(2,1)}, u32[]{:S(2)}, u32[]{:S(2)}) %collective-permute-start.5) | collective-permute-done | bytes 1048608 | tf_op jit(solution)/shard_map/ppermute | solution.py:53
  93.7 19.6 %collective-permute-done.6 = bf16[1024,512]{1,0:T(8,128)(2,1)S(1)} collective-permute-done((bf16[1024,512]{1,0:T(8,128)(2,1)S(1)}, bf16[1024,512]{1,0:T(8,128)(2,1)S(1)}, u32[]{:S(2)}, u32[]{:S(2)}) %collective-permute-start.6) | collective-permute-done | bytes 1048608 | tf_op jit(solution)/shard_map/ppermute | solution.py:51
  116.4 2.0 %fusion.6 = bf16[512,512]{1,0:T(8,128)(2,1)S(1)} fusion(bf16[512,512]{1,0:T(8,128)(2,1)S(1)} %collective-permute-done.22, bf16[1024,512]{1,0:T(8,128)(2,1)} %collective-permute-done.20, bf16[1024,512]{1,0:T(8,128)(2,1)} %collective-permute-done.21, pred[]{:T(512)S(6)} %eq.20, bf16[1024,1024]{1,0:T(8,128)(2,1)S(1)} %multiply_convert_fusion, s32[]{:T(128)S(6)} %select_n.83), kind=kOutput, calls=%fused_computation.21 | convolution fusion | flops 538181632 | bytes 4194309 | tf_op jit(solution)/shard_map/dot_general | solution.py:17
  118.4 4.3 %collective-permute-start.23 = (bf16[512,512]{1,0:T(8,128)(2,1)S(1)}, bf16[512,512]{1,0:T(8,128)(2,1)S(1)}, u32[]{:S(2)}, u32[]{:S(2)}) collective-permute-start(bf16[512,512]{1,0:T(8,128)(2,1)S(1)} %fusion.6), channel_id=1, source_target_pairs={{16,0},{24,8},{17,1},{25,9},{18,2},{26,10},{19,3},{27,11},{20,4},{... | collective-permute-start | bytes 1572872 | tf_op jit(solution)/shard_map/ppermute | solution.py:69
  122.7 2.0 %convolution_convert_fusion.1 = bf16[512,512]{1,0:T(8,128)(2,1)S(1)} fusion(bf16[1024,512]{1,0:T(8,128)(2,1)S(1)} %collective-permute-done.24, bf16[1024,512]{1,0:T(8,128)(2,1)} %collective-permute-done.20, pred[]{:T(512)S(6)} %eq.20, bf16[1024,1024]{1,0:T(8,128)(2,1)S(1)} %multiply_convert_fusion, s32[]{:T(128)S(6)} %select_n.84), kind=kOutput, calls=%fused_computation.23 | convolution fusion | flops 537657344 | bytes 3670021 | tf_op jit(solution)/shard_map/dot_general | solution.py:17
  129.1 2.1 %collective-permute-start.8 = (bf16[512,512]{1,0:T(8,128)(2,1)}, bf16[512,512]{1,0:T(8,128)(2,1)}, u32[]{:S(2)}, u32[]{:S(2)}) collective-permute-start(bf16[512,512]{1,0:T(8,128)(2,1)} %fusion.1), channel_id=1, source_target_pairs={{16,0},{24,8},{17,1},{25,9},{18,2},{26,10},{19,3},{27,11},{20,4},{... | collective-permute-start | bytes 1572872 | tf_op jit(solution)/shard_map/ppermute | solution.py:69
  131.1 2.8 %fusion.7 = bf16[512,512]{1,0:T(8,128)(2,1)} fusion(bf16[512,512]{1,0:T(8,128)(2,1)S(1)} %collective-permute-done.25, bf16[1024,512]{1,0:T(8,128)(2,1)S(1)} %collective-permute-done.24, bf16[1024,512]{1,0:T(8,128)(2,1)} %collective-permute-done.20, pred[]{:T(512)S(6)} %eq.20, bf16[1024,1024]{1,0:T(8,128)(2,1)S(1)} %multiply_convert_fusion, s32[]{:T(128)S(6)} %select_n.83), kind=kOutput, calls=%fused_computation.22 | convolution fusion | flops 538181632 | bytes 4194309 | tf_op jit(solution)/shard_map/dot_general | solution.py:17
  135.2 2.8 %fusion.4 = bf16[512,512]{1,0:T(8,128)(2,1)} fusion(bf16[512,512]{1,0:T(8,128)(2,1)S(1)} %collective-permute-done.15, bf16[1024,512]{1,0:T(8,128)(2,1)S(1)} %collective-permute-done.14, bf16[1024,512]{1,0:T(8,128)(2,1)} %collective-permute-done.5, pred[]{:T(512)S(6)} %eq.20, bf16[1024,1024]{1,0:T(8,128)(2,1)S(1)} %multiply_convert_fusion, s32[]{:T(128)S(6)} %select_n.83), kind=kOutput, calls=%fused_computation.19 | convolution fusion | flops 538181632 | bytes 4194309 | tf_op jit(solution)/shard_map/dot_general | solution.py:17
  139.4 2.8 %convolution_convert_fusion.6 = bf16[512,512]{1,0:T(8,128)(2,1)} fusion(bf16[1024,512]{1,0:T(8,128)(2,1)} %collective-permute-done.9, bf16[1024,1024]{1,0:T(8,128)(2,1)S(1)} %multiply_convert_fusion, s32[]{:T(128)S(6)} %select_n.84), kind=kOutput, calls=%fused_computation.28 | convolution fusion | flops 537133056 | bytes 2621444 | tf_op jit(solution)/shard_map/dot_general | solution.py:17
  142.5 2.8 %convolution_convert_fusion.3 = bf16[512,512]{1,0:T(8,128)(2,1)} fusion(bf16[1024,512]{1,0:T(8,128)(2,1)} %collective-permute-done.17, bf16[1024,1024]{1,0:T(8,128)(2,1)S(1)} %multiply_convert_fusion, s32[]{:T(128)S(6)} %select_n.84), kind=kOutput, calls=%fused_computation.25 | convolution fusion | flops 537133056 | bytes 2621444 | tf_op jit(solution)/shard_map/dot_general | solution.py:17
  147.4 2.0 %add.79 = bf16[512,1024]{1,0:T(8,128)(2,1)S(1)} add(bf16[512,1024]{1,0:T(8,128)(2,1)} %copy-done.7, bf16[512,1024]{1,0:T(8,128)(2,1)} %copy-done.8) | non-fusion elementwise | flops 524288 | bytes 3145728 | tf_op jit(solution)/shard_map/add | solution.py:69
  153.9 6.7 %collective-permute-done.16 = bf16[512,512]{1,0:T(8,128)(2,1)} collective-permute-done((bf16[512,512]{1,0:T(8,128)(2,1)}, bf16[512,512]{1,0:T(8,128)(2,1)}, u32[]{:S(2)}, u32[]{:S(2)}) %collective-permute-start.16) | collective-permute-done | bytes 524320 | tf_op jit(solution)/shard_map/ppermute | solution.py:69
  164.7 2.1 %fusion.2 = bf16[512,512]{1,0:T(8,128)(2,1)S(1)} fusion(bf16[1024,512]{1,0:T(8,128)(2,1)} %collective-permute-done.9, bf16[512,512]{1,0:T(8,128)(2,1)} %collective-permute-done.10, bf16[1024,1024]{1,0:T(8,128)(2,1)S(1)} %multiply_convert_fusion, s32[]{:T(128)S(6)} %select_n.83), kind=kOutput, calls=%fused_computation.17 | convolution fusion | flops 537657344 | bytes 3145732 | tf_op jit(solution)/shard_map/dot_general | solution.py:17
  166.8 2.1 %collective-permute-start.11 = (bf16[512,512]{1,0:T(8,128)(2,1)S(1)}, bf16[512,512]{1,0:T(8,128)(2,1)}, u32[]{:S(2)}, u32[]{:S(2)}) collective-permute-start(bf16[512,512]{1,0:T(8,128)(2,1)S(1)} %fusion.2), channel_id=1, source_target_pairs={{0,16},{24,8},{1,17},{25,9},{2,18},{26,10},{3,19},{27,11},{4,20},{... | collective-permute-start | bytes 1572872 | tf_op jit(solution)/shard_map/ppermute | solution.py:69
  168.9 2.9 %fusion.5 = bf16[512,512]{1,0:T(8,128)(2,1)} fusion(bf16[1024,512]{1,0:T(8,128)(2,1)} %collective-permute-done.17, bf16[512,512]{1,0:T(8,128)(2,1)} %collective-permute-done.18, bf16[1024,1024]{1,0:T(8,128)(2,1)S(1)} %multiply_convert_fusion, s32[]{:T(128)S(6)} %select_n.83), kind=kOutput, calls=%fused_computation.20 | convolution fusion | flops 537657344 | bytes 3145732 | tf_op jit(solution)/shard_map/dot_general | solution.py:17
  175.5 7.4 %collective-permute-done.19 = bf16[512,512]{1,0:T(8,128)(2,1)} collective-permute-done((bf16[512,512]{1,0:T(8,128)(2,1)}, bf16[512,512]{1,0:T(8,128)(2,1)}, u32[]{:S(2)}, u32[]{:S(2)}) %collective-permute-start.19) | collective-permute-done | bytes 524320 | tf_op jit(solution)/shard_map/ppermute | solution.py:69
  184.3 2.1 %broadcast_select_fusion.6 = (bf16[512,1024]{1,0:T(8,128)(2,1)S(1)}, bf16[512,1024]{1,0:T(8,128)(2,1)S(1)}) fusion(bf16[512,1024]{1,0:T(8,128)(2,1)} %collective-permute-done.27, pred[]{:T(512)S(6)} %eq.18, bf16[512,512]{1,0:T(8,128)(2,1)S(1)} %add.90, bf16[512,512]{1,0:T(8,128)(2,1)S(1)} %copy-done.6, bf16[512,512]{1,0:T(8,128)(2,1)S(1)} %copy-done.4, ...), kind=kLoop, calls=%fused_computation.41 | loop fusion | flops 8388608 | bytes 6815748 | tf_op jit(solution)/shard_map/jit(_where)/select_n | solution.py:100
  186.6 2.4 %maximum_convert_fusion = f32[1024,1024]{1,0:T(8,128)} fusion(bf16[512,1024]{1,0:T(8,128)(2,1)S(1)} %broadcast_select_fusion.5, bf16[512,1024]{1,0:T(8,128)(2,1)S(1)} %get-tuple-element.8), kind=kLoop, calls=%fused_computation.3 | loop fusion | flops 4194304 | bytes 6291456 | tf_op jit(solution)/shard_map/convert_element_type | solution.py:102
  (97 shorter events, 44.8 us)
Async XLA Ops:
  3.3 1.6 collective-permute-start
  4.9 2.7 %collective-permute-start.1 = (f32[3,1024]{1,0:T(4,128)S(1)}, f32[3,1024]{1,0:T(4,128)S(1)}, u32[]{:S(2)}, u32[]{:S(2)}) collective-permute-start(f32[3,1024]{1,0:T(4,128)S(1)} %fusion.46), channel_id=1, source_target_pairs={{0,16},{8,24},{16,0},{24,8},{1,17},{9,25},{17,1},{25,9},{2,18},{10... | collective-permute-start | bytes 36872 | tf_op jit(solution)/shard_map/ppermute | solution.py:13
  9.6 23.4 %collective-permute-start.9 = (bf16[1024,512]{1,0:T(8,128)(2,1)}, bf16[1024,512]{1,0:T(8,128)(2,1)}, u32[]{:S(2)}, u32[]{:S(2)}) collective-permute-start(bf16[1024,512]{1,0:T(8,128)(2,1)} %get-tuple-element.12), channel_id=1, source_target_pairs={{2,0},{3,1},{4,2},{5,3},{6,4},{7,5},{10,8},{11,9},{12,10},{13,11},... | collective-permute-start | bytes 3145736 | tf_op jit(solution)/shard_map/ppermute | solution.py:48
  12.7 42.7 %collective-permute-start.4 = (bf16[1024,512]{1,0:T(8,128)(2,1)S(1)}, bf16[1024,512]{1,0:T(8,128)(2,1)}, u32[]{:S(2)}, u32[]{:S(2)}) collective-permute-start(bf16[1024,512]{1,0:T(8,128)(2,1)S(1)} %get-tuple-element.13), channel_id=1, source_target_pairs={{2,0},{3,1},{4,2},{5,3},{6,4},{7,5},{10,8},{11,9},{12,10},{13,11},... | collective-permute-start | bytes 3145736 | tf_op jit(solution)/shard_map/ppermute | solution.py:50
  17.2 39.4 %collective-permute-start.2 = (bf16[512,1024]{1,0:T(8,128)(2,1)}, bf16[512,1024]{1,0:T(8,128)(2,1)}, u32[]{:S(2)}, u32[]{:S(2)}) collective-permute-start(bf16[512,1024]{1,0:T(8,128)(2,1)} %convolution_convert_fusion), channel_id=1, source_target_pairs={{0,8},{8,0},{16,24},{24,16},{1,9},{9,1},{17,25},{25,17},{2,10},{10... | collective-permute-start | bytes 3145736 | tf_op jit(solution)/shard_map/ppermute | solution.py:65
  19.1 40.8 %collective-permute-start.21 = (bf16[1024,512]{1,0:T(8,128)(2,1)}, bf16[1024,512]{1,0:T(8,128)(2,1)}, u32[]{:S(2)}, u32[]{:S(2)}) collective-permute-start(bf16[1024,512]{1,0:T(8,128)(2,1)} %get-tuple-element.12), channel_id=1, source_target_pairs={{1,0},{3,2},{5,4},{7,6},{9,8},{11,10},{13,12},{15,14},{17,16},{19,... | collective-permute-start | bytes 3145736 | tf_op jit(solution)/shard_map/ppermute | solution.py:49
  33.0 35.5 %collective-permute-start.20 = (bf16[1024,512]{1,0:T(8,128)(2,1)}, bf16[1024,512]{1,0:T(8,128)(2,1)}, u32[]{:S(2)}, u32[]{:S(2)}) collective-permute-start(bf16[1024,512]{1,0:T(8,128)(2,1)} %collective-permute-done.9), channel_id=1, source_target_pairs={{0,1},{2,3},{4,5},{6,7},{1,0},{3,2},{5,4},{7,6},{8,9},{10,11},{12,... | collective-permute-start | bytes 3145736 | tf_op jit(solution)/shard_map/ppermute | solution.py:52
  34.2 43.7 %collective-permute-start.17 = (bf16[1024,512]{1,0:T(8,128)(2,1)}, bf16[1024,512]{1,0:T(8,128)(2,1)}, u32[]{:S(2)}, u32[]{:S(2)}) collective-permute-start(bf16[1024,512]{1,0:T(8,128)(2,1)} %collective-permute-done.9), channel_id=1, source_target_pairs={{2,0},{3,1},{4,2},{5,3},{6,4},{7,5},{10,8},{11,9},{12,10},{13,11},... | collective-permute-start | bytes 3145736 | tf_op jit(solution)/shard_map/ppermute | solution.py:54
  55.4 35.6 %collective-permute-start.5 = (bf16[1024,512]{1,0:T(8,128)(2,1)}, bf16[1024,512]{1,0:T(8,128)(2,1)}, u32[]{:S(2)}, u32[]{:S(2)}) collective-permute-start(bf16[1024,512]{1,0:T(8,128)(2,1)} %collective-permute-done.4), channel_id=1, source_target_pairs={{0,1},{2,3},{4,5},{6,7},{1,0},{3,2},{5,4},{7,6},{8,9},{10,11},{12,... | collective-permute-start | bytes 3145736 | tf_op jit(solution)/shard_map/ppermute | solution.py:53
  56.6 56.7 %collective-permute-start.6 = (bf16[1024,512]{1,0:T(8,128)(2,1)S(1)}, bf16[1024,512]{1,0:T(8,128)(2,1)S(1)}, u32[]{:S(2)}, u32[]{:S(2)}) collective-permute-start(bf16[1024,512]{1,0:T(8,128)(2,1)S(1)} %get-tuple-element.13), channel_id=1, source_target_pairs={{1,0},{3,2},{5,4},{7,6},{9,8},{11,10},{13,12},{15,14},{17,16},{19,... | collective-permute-start | bytes 3145736 | tf_op jit(solution)/shard_map/ppermute | solution.py:51
  59.9 23.3 %collective-permute-start.12 = (bf16[512,512]{1,0:T(8,128)(2,1)S(1)}, bf16[512,512]{1,0:T(8,128)(2,1)S(1)}, u32[]{:S(2)}, u32[]{:S(2)}) collective-permute-start(bf16[512,512]{1,0:T(8,128)(2,1)S(1)} %convolution_convert_fusion.5), channel_id=1, source_target_pairs={{0,8},{8,0},{16,24},{24,16},{1,9},{9,1},{17,25},{25,17},{2,10},{10... | collective-permute-start | bytes 1572872 | tf_op jit(solution)/shard_map/ppermute | solution.py:65
  67.0 16.1 %copy-start.7 = (bf16[512,1024]{1,0:T(8,128)(2,1)}, bf16[512,1024]{1,0:T(8,128)(2,1)S(1)}, u32[]{:S(2)}) copy-start(bf16[512,1024]{1,0:T(8,128)(2,1)S(1)} %add_convert_fusion) | copy-start | bytes 3145732
  68.5 69.6 %collective-permute-start.3 = (bf16[512,1024]{1,0:T(8,128)(2,1)S(1)}, bf16[512,1024]{1,0:T(8,128)(2,1)S(1)}, u32[]{:S(2)}, u32[]{:S(2)}) collective-permute-start(bf16[512,1024]{1,0:T(8,128)(2,1)S(1)} %add_convert_fusion), channel_id=1, source_target_pairs={{16,0},{24,8},{17,1},{25,9},{18,2},{26,10},{19,3},{27,11},{20,4},{... | collective-permute-start | bytes 3145736 | tf_op jit(solution)/shard_map/ppermute | solution.py:69
  77.9 40.5 %collective-permute-start.24 = (bf16[1024,512]{1,0:T(8,128)(2,1)}, bf16[1024,512]{1,0:T(8,128)(2,1)S(1)}, u32[]{:S(2)}, u32[]{:S(2)}) collective-permute-start(bf16[1024,512]{1,0:T(8,128)(2,1)} %collective-permute-done.17), channel_id=1, source_target_pairs={{0,1},{2,3},{4,5},{6,7},{8,9},{10,11},{12,13},{14,15},{16,17},{18,... | collective-permute-start | bytes 3145736 | tf_op jit(solution)/shard_map/ppermute | solution.py:55
  83.2 32.3 %collective-permute-start.22 = (bf16[512,512]{1,0:T(8,128)(2,1)S(1)}, bf16[512,512]{1,0:T(8,128)(2,1)S(1)}, u32[]{:S(2)}, u32[]{:S(2)}) collective-permute-start(bf16[512,512]{1,0:T(8,128)(2,1)S(1)} %convolution_convert_fusion.2), channel_id=1, source_target_pairs={{0,8},{8,0},{16,24},{24,16},{1,9},{9,1},{17,25},{25,17},{2,10},{10... | collective-permute-start | bytes 1572872 | tf_op jit(solution)/shard_map/ppermute | solution.py:65
  91.0 33.8 %collective-permute-start.14 = (bf16[1024,512]{1,0:T(8,128)(2,1)}, bf16[1024,512]{1,0:T(8,128)(2,1)S(1)}, u32[]{:S(2)}, u32[]{:S(2)}) collective-permute-start(bf16[1024,512]{1,0:T(8,128)(2,1)} %collective-permute-done.5), channel_id=1, source_target_pairs={{3,1},{5,3},{7,5},{11,9},{13,11},{15,13},{19,17},{21,19},{23,21},{... | collective-permute-start | bytes 3145736 | tf_op jit(solution)/shard_map/ppermute | solution.py:56
  93.7 21.7 %copy-start.9 = (bf16[512,512]{1,0:T(8,128)(2,1)}, bf16[512,512]{1,0:T(8,128)(2,1)S(1)}, u32[]{:S(2)}) copy-start(bf16[512,512]{1,0:T(8,128)(2,1)S(1)} %fusion.3) | copy-start | bytes 1572868
  113.3 28.9 %collective-permute-start.13 = (bf16[512,512]{1,0:T(8,128)(2,1)S(1)}, bf16[512,512]{1,0:T(8,128)(2,1)S(1)}, u32[]{:S(2)}, u32[]{:S(2)}) collective-permute-start(bf16[512,512]{1,0:T(8,128)(2,1)S(1)} %fusion.3), channel_id=1, source_target_pairs={{0,16},{8,24},{1,17},{9,25},{2,18},{10,26},{3,19},{11,27},{4,20},{... | collective-permute-start | bytes 1572872 | tf_op jit(solution)/shard_map/ppermute | solution.py:69
  115.4 11.7 %collective-permute-start.7 = (bf16[512,512]{1,0:T(8,128)(2,1)S(1)}, bf16[512,512]{1,0:T(8,128)(2,1)S(1)}, u32[]{:S(2)}, u32[]{:S(2)}) collective-permute-start(bf16[512,512]{1,0:T(8,128)(2,1)S(1)} %convolution_convert_fusion.7), channel_id=1, source_target_pairs={{0,8},{8,0},{16,24},{24,16},{1,9},{9,1},{17,25},{25,17},{2,10},{10... | collective-permute-start | bytes 1572872 | tf_op jit(solution)/shard_map/ppermute | solution.py:65
  118.4 26.9 %collective-permute-start.23 = (bf16[512,512]{1,0:T(8,128)(2,1)S(1)}, bf16[512,512]{1,0:T(8,128)(2,1)S(1)}, u32[]{:S(2)}, u32[]{:S(2)}) collective-permute-start(bf16[512,512]{1,0:T(8,128)(2,1)S(1)} %fusion.6), channel_id=1, source_target_pairs={{16,0},{24,8},{17,1},{25,9},{18,2},{26,10},{19,3},{27,11},{20,4},{... | collective-permute-start | bytes 1572872 | tf_op jit(solution)/shard_map/ppermute | solution.py:69
  124.8 4.3 %collective-permute-start.25 = (bf16[512,512]{1,0:T(8,128)(2,1)S(1)}, bf16[512,512]{1,0:T(8,128)(2,1)S(1)}, u32[]{:S(2)}, u32[]{:S(2)}) collective-permute-start(bf16[512,512]{1,0:T(8,128)(2,1)S(1)} %convolution_convert_fusion.1), channel_id=1, source_target_pairs={{0,8},{8,0},{16,24},{24,16},{1,9},{9,1},{17,25},{25,17},{2,10},{10... | collective-permute-start | bytes 1572872 | tf_op jit(solution)/shard_map/ppermute | solution.py:65
  127.1 6.8 %collective-permute-start.15 = (bf16[512,512]{1,0:T(8,128)(2,1)S(1)}, bf16[512,512]{1,0:T(8,128)(2,1)S(1)}, u32[]{:S(2)}, u32[]{:S(2)}) collective-permute-start(bf16[512,512]{1,0:T(8,128)(2,1)S(1)} %convolution_convert_fusion.4), channel_id=1, source_target_pairs={{0,8},{8,0},{16,24},{24,16},{1,9},{9,1},{17,25},{25,17},{2,10},{10... | collective-permute-start | bytes 1572872 | tf_op jit(solution)/shard_map/ppermute | solution.py:65
  129.1 22.1 %collective-permute-start.8 = (bf16[512,512]{1,0:T(8,128)(2,1)}, bf16[512,512]{1,0:T(8,128)(2,1)}, u32[]{:S(2)}, u32[]{:S(2)}) collective-permute-start(bf16[512,512]{1,0:T(8,128)(2,1)} %fusion.1), channel_id=1, source_target_pairs={{16,0},{24,8},{17,1},{25,9},{18,2},{26,10},{19,3},{27,11},{20,4},{... | collective-permute-start | bytes 1572872 | tf_op jit(solution)/shard_map/ppermute | solution.py:69
  134.0 18.6 %collective-permute-start.26 = (bf16[512,512]{1,0:T(8,128)(2,1)}, bf16[512,512]{1,0:T(8,128)(2,1)}, u32[]{:S(2)}, u32[]{:S(2)}) collective-permute-start(bf16[512,512]{1,0:T(8,128)(2,1)} %fusion.7), channel_id=1, source_target_pairs={{0,16},{8,24},{1,17},{9,25},{2,18},{10,26},{3,19},{11,27},{4,20},{... | collective-permute-start | bytes 1572872 | tf_op jit(solution)/shard_map/ppermute | solution.py:69
  138.1 22.5 %collective-permute-start.16 = (bf16[512,512]{1,0:T(8,128)(2,1)}, bf16[512,512]{1,0:T(8,128)(2,1)}, u32[]{:S(2)}, u32[]{:S(2)}) collective-permute-start(bf16[512,512]{1,0:T(8,128)(2,1)} %fusion.4), channel_id=1, source_target_pairs={{0,16},{8,24},{1,17},{9,25},{2,18},{10,26},{3,19},{11,27},{4,20},{... | collective-permute-start | bytes 1572872 | tf_op jit(solution)/shard_map/ppermute | solution.py:69
  142.2 22.5 %collective-permute-start.10 = (bf16[512,512]{1,0:T(8,128)(2,1)}, bf16[512,512]{1,0:T(8,128)(2,1)}, u32[]{:S(2)}, u32[]{:S(2)}) collective-permute-start(bf16[512,512]{1,0:T(8,128)(2,1)} %convolution_convert_fusion.6), channel_id=1, source_target_pairs={{0,8},{8,0},{16,24},{24,16},{1,9},{9,1},{17,25},{25,17},{2,10},{10... | collective-permute-start | bytes 1572872 | tf_op jit(solution)/shard_map/ppermute | solution.py:65
  146.1 22.8 %collective-permute-start.18 = (bf16[512,512]{1,0:T(8,128)(2,1)}, bf16[512,512]{1,0:T(8,128)(2,1)}, u32[]{:S(2)}, u32[]{:S(2)}) collective-permute-start(bf16[512,512]{1,0:T(8,128)(2,1)} %convolution_convert_fusion.3), channel_id=1, source_target_pairs={{0,8},{16,24},{1,9},{17,25},{2,10},{18,26},{3,11},{19,27},{4,12},{... | collective-permute-start | bytes 1572872 | tf_op jit(solution)/shard_map/ppermute | solution.py:65
  163.6 20.7 %collective-permute-start.27 = (bf16[512,1024]{1,0:T(8,128)(2,1)}, bf16[512,1024]{1,0:T(8,128)(2,1)}, u32[]{:S(2)}, u32[]{:S(2)}) collective-permute-start(bf16[512,1024]{1,0:T(8,128)(2,1)} %fusion.9), channel_id=1, source_target_pairs={{0,8},{8,0},{16,24},{24,16},{1,9},{9,1},{17,25},{25,17},{2,10},{10... | collective-permute-start | bytes 3145736 | tf_op jit(solution)/shard_map/ppermute | solution.py:13
  166.8 7.4 %collective-permute-start.11 = (bf16[512,512]{1,0:T(8,128)(2,1)S(1)}, bf16[512,512]{1,0:T(8,128)(2,1)}, u32[]{:S(2)}, u32[]{:S(2)}) collective-permute-start(bf16[512,512]{1,0:T(8,128)(2,1)S(1)} %fusion.2), channel_id=1, source_target_pairs={{0,16},{24,8},{1,17},{25,9},{2,18},{26,10},{3,19},{27,11},{4,20},{... | collective-permute-start | bytes 1572872 | tf_op jit(solution)/shard_map/ppermute | solution.py:69
  171.8 12.5 %copy-start.4 = (bf16[512,512]{1,0:T(8,128)(2,1)S(1)}, bf16[512,512]{1,0:T(8,128)(2,1)}, u32[]{:S(2)}) copy-start(bf16[512,512]{1,0:T(8,128)(2,1)} %copy-done.3) | copy-start | bytes 1572868
  171.8 12.5 %copy-start.6 = (bf16[512,512]{1,0:T(8,128)(2,1)S(1)}, bf16[512,512]{1,0:T(8,128)(2,1)}, u32[]{:S(2)}) copy-start(bf16[512,512]{1,0:T(8,128)(2,1)} %copy-done.5) | copy-start | bytes 1572868
  171.8 11.1 %collective-permute-start.19 = (bf16[512,512]{1,0:T(8,128)(2,1)}, bf16[512,512]{1,0:T(8,128)(2,1)}, u32[]{:S(2)}, u32[]{:S(2)}) collective-permute-start(bf16[512,512]{1,0:T(8,128)(2,1)} %fusion.5), channel_id=1, source_target_pairs={{8,24},{9,25},{10,26},{11,27},{12,28},{13,29},{14,30},{15,31}} | collective-permute-start | bytes 1572872 | tf_op jit(solution)/shard_map/ppermute | solution.py:69
  (15 other events, 71.7 us)

commit v2 on v1

v2 whole, which is shorter than its diff:
```python
import jax
import jax.numpy as jnp
from jax import lax
from jax.experimental import pallas as pl
from jax.experimental.pallas import tpu as pltpu
from jax.sharding import PartitionSpec as P

TILE = 512
BAND = 4096
EPS = 1e-05
MESH = pl.DeviceIdType.MESH


def exchanged(x, axis, mask):
    count = lax.axis_size(axis)
    return lax.ppermute(x, axis, [(i, i ^ mask) for i in range(count)])


def band_kernel(
    count, own, keep_rows, send_rows, out,
    panels, given, got, part, far, passed,
    panel_send, panel_recv, given_send, got_recv, part_send, far_recv, final_send, final_recv,
):
    p, samp = lax.axis_index("snp"), lax.axis_index("samp")
    core, x = samp % 2, samp // 2
    core_peer = samp + 1 - 2 * core
    x_peer = samp + 2 - 4 * x
    odd = p % 2 == 1
    even = p % 2 == 0
    mate = p + 1 - 2 * (p % 2)
    has_down = p >= 2
    has_up = p + 2 < count

    barrier = pltpu.get_barrier_semaphore()

    def greet(where):
        pl.semaphore_signal(barrier, inc=1, device_id=where, device_id_type=MESH)

    greet({"samp": core_peer})
    greet({"samp": x_peer})
    greet({"snp": mate})

    @pl.when(has_down)
    def _():
        greet({"snp": p - 2})

    @pl.when(has_up)
    def _():
        greet({"snp": p + 2})

    peers = 3 + has_down.astype(jnp.int32) + has_up.astype(jnp.int32)
    pl.semaphore_wait(barrier, peers)

    def block(h):
        return own.at[h] if h < 2 else panels.at[h - 2]

    def valid(h):
        return p + h // 2 < count

    def panel_copy(n, source, target, where):
        return pltpu.make_async_remote_copy(
            src_ref=block(source), dst_ref=panels.at[target - 2],
            send_sem=panel_send.at[n], recv_sem=panel_recv.at[target - 2],
            device_id={"snp": where}, device_id_type=MESH,
        )

    sends = {
        "z0": (0, has_down, 0, 4, p - 2),
        "z1": (1, has_down, 1, 5, p - 2),
        "a0": (2, odd, 0, 2, mate),
        "a1": (3, odd, 1, 3, mate),
        "y0e": (4, even & has_up, 4, 2, mate),
        "y0o": (4, odd & has_up, 4, 6, mate),
        "y1e": (5, even & has_up, 5, 3, mate),
        "y1o": (5, odd & has_up, 5, 7, mate),
        "d0": (6, has_down & has_up, 4, 8, p - 2),
        "e0": (7, even & (p + 4 < count), 8, 6, mate),
        "e1": (8, odd & has_down & (p + 1 < count), 3, 7, p - 2),
    }

    def send(name):
        n, cond, source, target, where = sends[name]

        @pl.when(cond)
        def _():
            panel_copy(n, source, target, where).start()

    def arrived(h):
        @pl.when(valid(h))
        def _():
            panel_copy(0, 0, h, mate).wait_recv()

    def keeps(h):
        return valid(h) & {0: core == 0, 8: core == 1}.get(h, core >= 0)

    def gives(h):
        return valid(h) & {0: core == 1, 8: core == 0}.get(h, core >= 0)

    def given_copy(h):
        return pltpu.make_async_remote_copy(
            src_ref=given.at[h], dst_ref=got.at[h],
            send_sem=given_send.at[h], recv_sem=got_recv.at[h],
            device_id={"samp": core_peer}, device_id_type=MESH,
        )

    def part_copy(h):
        return pltpu.make_async_remote_copy(
            src_ref=part.at[h], dst_ref=far.at[h],
            send_sem=part_send.at[h], recv_sem=far_recv.at[h],
            device_id={"samp": x_peer}, device_id_type=MESH,
        )

    step = 256
    steps = keep_rows.shape[0] // step

    def first(h):
        @pl.when(gives(h))
        def _():
            @pl.loop(0, steps)
            def _(r):
                rows = pl.ds(pl.multiple_of(r * step, step), step)
                given[h, rows, :] = jnp.dot(
                    send_rows[rows, :], block(h)[...], preferred_element_type=jnp.float32
                ).astype(given.dtype)

            given_copy(h).start()

    def owner(h):
        return (h - core) // 4

    def second(h):
        @pl.when(keeps(h))
        def _():
            given_copy(h).wait_recv()

            @pl.loop(0, steps)
            def _(r):
                rows = pl.ds(pl.multiple_of(r * step, step), step)
                value = jnp.dot(
                    keep_rows[rows, :], block(h)[...], preferred_element_type=jnp.float32
                )
                part[h, rows, :] = (value + got[h, rows, :].astype(jnp.float32)).astype(part.dtype)

            @pl.when(owner(h) != x)
            def _():
                part_copy(h).start()

    def final_copy(j):
        return pltpu.make_async_remote_copy(
            src_ref=passed.at[j], dst_ref=out.at[core, j],
            send_sem=final_send.at[j], recv_sem=final_recv.at[j],
            device_id={"samp": core_peer}, device_id_type=MESH,
        )

    def third(h):
        for c in (0, 1):
            i = (h - c) % 4
            j = i % 2
            stays = (i < 2) == (c == 0)
            if not 0 <= h - c < 8:
                continue
            mine = (core == c) & (owner(h) == x)

            def total(target, at, i=i):
                @pl.when(mine & valid(h))
                def _():
                    part_copy(h).wait_recv()
                    target[at] = (
                        part[h].astype(jnp.float32) + far[h].astype(jnp.float32)
                    ).astype(target.dtype)

                @pl.when(mine & jnp.logical_not(valid(h)))
                def _():
                    target[at] = jnp.zeros(target.shape[-2:], target.dtype)

            if stays:
                total(out, (c, j))
            else:
                total(passed, (j,))

                @pl.when(mine)
                def _(j=j):
                    final_copy(j).start()

    for name in ("z0", "a0", "z1", "a1"):
        send(name)
    first(0)
    first(1)
    second(0)
    second(1)
    arrived(4)
    for name in ("y0e", "y0o", "d0"):
        send(name)
    first(4)
    second(4)
    arrived(5)
    for name in ("y1e", "y1o"):
        send(name)
    first(5)
    second(5)
    arrived(2)
    first(2)
    second(2)
    arrived(3)
    send("e1")
    first(3)
    arrived(8)
    send("e0")
    first(8)
    second(3)
    second(8)
    for h in (0, 1, 2):
        third(h)
    arrived(6)
    first(6)
    second(6)
    arrived(7)
    first(7)
    second(7)
    for h in (3, 4, 5, 8, 6, 7):
        third(h)

    for j in (0, 1):
        final_copy(j).wait_recv()
        final_copy(j).wait_send()
    for n, cond, source, target, where in sends.values():
        @pl.when(cond)
        def _(n=n, source=source, target=target, where=where):
            panel_copy(n, source, target, where).wait_send()
    for h in range(9):
        @pl.when(gives(h))
        def _(h=h):
            given_copy(h).wait_send()

        @pl.when(keeps(h) & (owner(h) != x))
        def _(h=h):
            part_copy(h).wait_send()


def on_device(genotypes):
    present = (genotypes >= 0).astype(jnp.float32)
    dosage = genotypes * present
    stats = jnp.stack(
        [jnp.sum(present, axis=0), jnp.sum(dosage, axis=0), jnp.sum(dosage * dosage, axis=0)]
    )
    stats = stats + exchanged(stats, "samp", 1)
    stats = stats + exchanged(stats, "samp", 2)
    counted, summed, squared = stats[0], stats[1], stats[2]
    average = summed / counted
    spread = squared / counted - average * average
    col_norms = counted * spread / (spread + EPS)
    factor = lax.rsqrt(spread + EPS) * lax.rsqrt(col_norms)
    scaled = (present * (dosage - average) * factor).astype(jnp.bfloat16)

    samples, snps = genotypes.shape
    half = snps // 2
    count = lax.axis_size("snp")
    assert half == TILE and BAND == 8 * half
    assert count % 2 == 0 and lax.axis_size("samp") == 4
    core = lax.axis_index("samp") % 2
    own = jnp.stack([scaled[:, :half], scaled[:, half:]])
    flipped = scaled.T
    keep_rows = lax.dynamic_slice_in_dim(flipped, core * half, half, 0)
    send_rows = lax.dynamic_slice_in_dim(flipped, (1 - core) * half, half, 0)

    piece = lambda n: pltpu.VMEM((n, half, half), jnp.bfloat16)
    sems = lambda n: pltpu.SemaphoreType.DMA((n,))
    vmem = pl.BlockSpec(memory_space=pltpu.VMEM)
    out = pl.pallas_call(
        lambda *refs: band_kernel(count, *refs),
        out_shape=jax.ShapeDtypeStruct((2, 2, half, half), jnp.bfloat16),
        in_specs=[vmem] * 3,
        out_specs=vmem,
        scratch_shapes=[
            pltpu.VMEM((7, samples, half), jnp.bfloat16),
            piece(9), piece(9), piece(9), piece(9), piece(2),
            sems(9), sems(7), sems(9), sems(9), sems(9), sems(9), sems(2), sems(2),
        ],
        compiler_params=pltpu.CompilerParams(
            collective_id=0, has_side_effects=True, vmem_limit_bytes=60 * 1024 * 1024
        ),
    )(own, keep_rows, send_rows)
    return out.transpose(0, 2, 1, 3).reshape(snps, snps).astype(jnp.float32)


def solution(mesh):
    return jax.shard_map(
        on_device, mesh=mesh, in_specs=(P("samp", "snp"),), out_specs=P("snp", "samp"),
        check_vma=False,
    )
```

time: 190 us -> 154 us (0.81)
  the two profiles are of different devices: /device:TPU:27 before, /device:TPU:15 now
where the time goes in v2:
time: 154 us
  Pallas kernels  125 us (81%)
  local copies, waits for them, and re-layouts  15.9 us (10%)
  other arithmetic  9.02 us (6%)
  waiting for transfers between devices  3.17 us (2%)
    pallas_call x1, Pallas kernels, on_device(): pl.pallas_call(lambda *refs: band_kernel(count, *refs), out_shape=jax.Sha...  125 us
    unnamed x2, local copies, waits for them, and re-layouts  8.35 us
    reduce_sum x1, other arithmetic, on_device(): jnp.sum(present, axis=0)  3.56 us
    convert_element_type x1, local copies, waits for them, and re-layouts, on_device(): return out.transpose(0, 2, 1, 3).reshape(snps, snps).astype(jnp.float32)  3.24 us
    ppermute x2, waiting for transfers between devices, exchanged(): return lax.ppermute(x, axis, [(i, i ^ mask) for i in range(count)])  3.17 us
  transfers between devices with their start and end apart: 2, of which 2 were waited for; matrix products, arithmetic and copies ran while one was open for 0% of the time, Pallas kernels for 0%

profile of v2, /device:TPU:15, one launch (start us, length us, event | category | flops | bytes accessed | tf_op | source)
XLA Modules:
  0.0 153.9 jit_solution(16071123537939636026)
XLA Ops:
  0.0 5.3 %copy.5 = f32[1024,1024]{0,1:T(8,128)} copy(f32[1024,1024]{1,0:T(8,128)} %param.1) | data formatting | bytes 8388608 | tf_op args[0]
  5.3 3.6 %convert_reduce_fusion = (f32[1024]{0:T(1024)S(1)}, f32[1024]{0:T(1024)S(1)}, f32[1024]{0:T(1024)S(1)}) fusion(f32[1024,1024]{0,1:T(8,128)} %copy.5), kind=kLoop, calls=%fused_computation.3 | loop fusion | flops 7336960 | bytes 4206592 | tf_op jit(solution)/shard_map/reduce_sum | solution.py:244
  8.9 0.7 collective-permute-start
  9.7 0.8 collective-permute-done
  10.5 0.3 collective-permute-start.1
  10.8 2.3 %collective-permute-done.1 = f32[3,1024]{1,0:T(4,128)S(1)} collective-permute-done((f32[3,1024]{1,0:T(4,128)S(1)}, f32[3,1024]{1,0:T(4,128)S(1)}, u32[]{:S(2)}, u32[]{:S(2)}) %collective-permute-start.1) | collective-permute-done | bytes 12320 | tf_op jit(solution)/shard_map/ppermute | solution.py:16
  13.2 3.0 %multiply_convert_fusion = bf16[1024,1024]{0,1:T(8,128)(2,1)S(1)} fusion(f32[1024]{0:T(1024)S(1)} %bitcast.28, f32[1024]{0:T(1024)S(1)} %bitcast.29, f32[1024,1024]{0,1:T(8,128)} %copy.5), kind=kLoop, calls=%fused_computation.1 | loop fusion | flops 6291456 | bytes 6299648 | tf_op jit(solution)/shard_map/convert_element_type | solution.py:253
  16.3 1.7 %dynamic-slice_bitcast_fusion = (bf16[512,1024]{1,0:T(8,128)(2,1)}, bf16[512,1024]{1,0:T(8,128)(2,1)}, bf16[1,1024,512]{1,2,0:T(8,128)(2,1)S(1)}, bf16[1,1024,512]{1,2,0:T(8,128)(2,1)S(1)}) fusion(bf16[1024,1024]{0,1:T(8,128)(2,1)S(1)} %multiply_convert_fusion, s32[]{:T(128)S(6)} %select_n.15, s32[]{:T(128)S(6)} %select_n.14), kind=kLoop, calls=%fused_computation.10 | loop fusion | bytes 8388616 | tf_op jit(solution)/shard_map/dynamic_slice | solution.py:264
  18.0 0.2 pad_maximum_fusion
  18.2 2.6 %copy.7.refs_0_ = bf16[2,1024,512]{2,1,0:T(8,128)(2,1)} copy(bf16[2,1024,512]{1,2,0:T(8,128)(2,1)S(1)} %pad_maximum_fusion) | data formatting | bytes 4194304 | tf_op jit(solution)/shard_map/stack | solution.py:261
  20.8 124.7 %shard_map.17 = bf16[2,2,512,512]{3,2,1,0:T(8,128)(2,1)} custom-call(bf16[2,1024,512]{2,1,0:T(8,128)(2,1)} %copy.7.refs_0_, bf16[512,1024]{1,0:T(8,128)(2,1)} %get-tuple-element.11.refs_1_, bf16[512,1024]{1,0:T(8,128)(2,1)} %get-tuple-element.10.refs_2_), custom_call_target="tpu_custom_call" | custom-call | tf_op jit(solution)/shard_map/pallas_call | solution.py:269
  145.5 2.2 %convert_bitcast_fusion = f32[2,512,2,512]{3,1,2,0:T(8,128)S(1)} fusion(bf16[2,2,512,512]{3,2,1,0:T(8,128)(2,1)} %shard_map.17), kind=kLoop, calls=%fused_computation | loop fusion | flops 1048576 | bytes 6291456 | tf_op jit(solution)/shard_map/convert_element_type | solution.py:283
  147.7 3.2 %copy.8 = f32[2,512,2,512]{3,2,1,0:T(2,128)S(1)} copy(f32[2,512,2,512]{3,1,2,0:T(8,128)S(1)} %convert_bitcast_fusion) | data formatting | bytes 8388608 | tf_op jit(solution)/shard_map/convert_element_type | solution.py:283
  150.9 3.0 %copy.9 = f32[128,8,2,512]{3,1,2,0:T(8,128)} copy(f32[128,8,2,512]{3,2,1,0:T(2,128)S(1)} %bitcast.18) | data formatting | bytes 8388608
  (4 shorter events, 0.1 us)
Async XLA Ops:
  8.9 1.6 %collective-permute-start = (f32[3,1024]{1,0:T(4,128)S(1)}, f32[3,1024]{1,0:T(4,128)S(1)}, u32[]{:S(2)}, u32[]{:S(2)}) collective-permute-start(f32[3,1024]{1,0:T(4,128)S(1)} %pad_maximum_fusion.1), channel_id=1, source_target_pairs={{0,8},{8,0},{16,24},{24,16},{1,9},{9,1},{17,25},{25,17},{2,10},{10... | collective-permute-start | bytes 36872 | tf_op jit(solution)/shard_map/ppermute | solution.py:16
  10.5 2.7 %collective-permute-start.1 = (f32[3,1024]{1,0:T(4,128)S(1)}, f32[3,1024]{1,0:T(4,128)S(1)}, u32[]{:S(2)}, u32[]{:S(2)}) collective-permute-start(f32[3,1024]{1,0:T(4,128)S(1)} %fusion.2), channel_id=1, source_target_pairs={{0,16},{8,24},{16,0},{24,8},{1,17},{9,25},{17,1},{25,9},{2,18},{10... | collective-permute-start | bytes 36872 | tf_op jit(solution)/shard_map/ppermute | solution.py:16

commit v3 on v2

--- a/solution.py
+++ b/solution.py
@@ -110,8 +110,9 @@
             device_id={"samp": x_peer}, device_id_type=MESH,
         )
 
+    half = keep_rows.shape[0]
     step = 256
-    steps = keep_rows.shape[0] // step
+    steps = half // step
 
     def first(h):
         @pl.when(gives(h))
@@ -147,7 +148,7 @@
 
     def final_copy(j):
         return pltpu.make_async_remote_copy(
-            src_ref=passed.at[j], dst_ref=out.at[core, j],
+            src_ref=passed.at[j], dst_ref=out.at[core, :, pl.ds(j * half, half)],
             send_sem=final_send.at[j], recv_sem=final_recv.at[j],
             device_id={"samp": core_peer}, device_id_type=MESH,
         )
@@ -171,10 +172,10 @@
 
                 @pl.when(mine & jnp.logical_not(valid(h)))
                 def _():
-                    target[at] = jnp.zeros(target.shape[-2:], target.dtype)
+                    target[at] = jnp.zeros(part.shape[1:], target.dtype)
 
             if stays:
-                total(out, (c, j))
+                total(out, (c, slice(None), pl.ds(j * half, half)))
             else:
                 total(passed, (j,))
 
@@ -268,7 +269,7 @@
     vmem = pl.BlockSpec(memory_space=pltpu.VMEM)
     out = pl.pallas_call(
         lambda *refs: band_kernel(count, *refs),
-        out_shape=jax.ShapeDtypeStruct((2, 2, half, half), jnp.bfloat16),
+        out_shape=jax.ShapeDtypeStruct((2, half, snps), jnp.bfloat16),
         in_specs=[vmem] * 3,
         out_specs=vmem,
         scratch_shapes=[
@@ -280,7 +281,7 @@
             collective_id=0, has_side_effects=True, vmem_limit_bytes=60 * 1024 * 1024
         ),
     )(own, keep_rows, send_rows)
-    return out.transpose(0, 2, 1, 3).reshape(snps, snps).astype(jnp.float32)
+    return out.reshape(snps, snps).astype(jnp.float32)
 
 
 def solution(mesh):

time: 154 us -> 150 us (0.974)
  local copies, waits for them, and re-layouts: 15.9 us -> 9.65 us
  other arithmetic: 9.02 us -> 10.9 us
    convert_element_type x1 -> x0, local copies, waits for them, and re-layouts: 3.24 us -> none  [on_device(): return out.transpose(0, 2, 1, 3).reshape(snps, snps).astype(jnp.float32)]
    unnamed x2 -> x1, local copies, waits for them, and re-layouts: 8.35 us -> 5.34 us
    convert_element_type x1, other arithmetic: 2.17 us -> 4.07 us  [on_device(): return out.reshape(snps, snps).astype(jnp.float32)]
where the time goes in v3:
time: 150 us
  Pallas kernels  125 us (83%)
  other arithmetic  10.9 us (7%)
  local copies, waits for them, and re-layouts  9.65 us (6%)
  waiting for transfers between devices  3.17 us (2%)
    pallas_call x1, Pallas kernels, on_device(): pl.pallas_call(lambda *refs: band_kernel(count, *refs), out_shape=jax.Sha...  125 us
    unnamed x1, local copies, waits for them, and re-layouts  5.34 us
    convert_element_type x1, other arithmetic, on_device(): return out.reshape(snps, snps).astype(jnp.float32)  4.07 us
    reduce_sum x1, other arithmetic, on_device(): jnp.sum(present, axis=0)  3.56 us
    ppermute x2, waiting for transfers between devices, exchanged(): return lax.ppermute(x, axis, [(i, i ^ mask) for i in range(count)])  3.17 us
    convert_element_type x1, other arithmetic, on_device(): scaled = (present * (dosage - average) * factor).astype(jnp.bfloat16)  3.01 us
  transfers between devices with their start and end apart: 2, of which 2 were waited for; matrix products, arithmetic and copies ran while one was open for 0% of the time, Pallas kernels for 0%

profile of v3, /device:TPU:15, one launch (start us, length us, event | category | flops | bytes accessed | tf_op | source)
XLA Modules:
  0.0 149.6 jit_solution(796086972768751941)
XLA Ops:
  0.0 5.3 %copy.2 = f32[1024,1024]{0,1:T(8,128)} copy(f32[1024,1024]{1,0:T(8,128)} %param.1) | data formatting | bytes 8388608 | tf_op args[0]
  5.3 3.6 %convert_reduce_fusion = (f32[1024]{0:T(1024)S(1)}, f32[1024]{0:T(1024)S(1)}, f32[1024]{0:T(1024)S(1)}) fusion(f32[1024,1024]{0,1:T(8,128)} %copy.2), kind=kLoop, calls=%fused_computation.2 | loop fusion | flops 7336960 | bytes 4206592 | tf_op jit(solution)/shard_map/reduce_sum | solution.py:245
  8.9 0.7 collective-permute-start
  9.7 0.8 collective-permute-done
  10.5 0.3 collective-permute-start.1
  10.8 2.3 %collective-permute-done.1 = f32[3,1024]{1,0:T(4,128)S(1)} collective-permute-done((f32[3,1024]{1,0:T(4,128)S(1)}, f32[3,1024]{1,0:T(4,128)S(1)}, u32[]{:S(2)}, u32[]{:S(2)}) %collective-permute-start.1) | collective-permute-done | bytes 12320 | tf_op jit(solution)/shard_map/ppermute | solution.py:16
  13.2 3.0 %multiply_convert_fusion = bf16[1024,1024]{0,1:T(8,128)(2,1)S(1)} fusion(f32[1024]{0:T(1024)S(1)} %bitcast.25, f32[1024]{0:T(1024)S(1)} %bitcast.26, f32[1024,1024]{0,1:T(8,128)} %copy.2), kind=kLoop, calls=%fused_computation | loop fusion | flops 6291456 | bytes 6299648 | tf_op jit(solution)/shard_map/convert_element_type | solution.py:254
  16.3 1.7 %dynamic-slice_bitcast_fusion = (bf16[512,1024]{1,0:T(8,128)(2,1)}, bf16[512,1024]{1,0:T(8,128)(2,1)}, bf16[1,1024,512]{1,2,0:T(8,128)(2,1)S(1)}, bf16[1,1024,512]{1,2,0:T(8,128)(2,1)S(1)}) fusion(bf16[1024,1024]{0,1:T(8,128)(2,1)S(1)} %multiply_convert_fusion, s32[]{:T(128)S(6)} %select_n.15, s32[]{:T(128)S(6)} %select_n.14), kind=kLoop, calls=%fused_computation.10 | loop fusion | bytes 8388616 | tf_op jit(solution)/shard_map/dynamic_slice | solution.py:265
  18.0 0.2 pad_maximum_fusion
  18.2 2.6 %copy.4.refs_0_ = bf16[2,1024,512]{2,1,0:T(8,128)(2,1)} copy(bf16[2,1024,512]{1,2,0:T(8,128)(2,1)S(1)} %pad_maximum_fusion) | data formatting | bytes 4194304 | tf_op jit(solution)/shard_map/stack | solution.py:262
  20.8 124.7 %shard_map.17 = bf16[2,512,1024]{2,1,0:T(8,128)(2,1)} custom-call(bf16[2,1024,512]{2,1,0:T(8,128)(2,1)} %copy.4.refs_0_, bf16[512,1024]{1,0:T(8,128)(2,1)} %get-tuple-element.11.refs_1_, bf16[512,1024]{1,0:T(8,128)(2,1)} %get-tuple-element.10.refs_2_), custom_call_target="tpu_custom_call" | custom-call | tf_op jit(solution)/shard_map/pallas_call | solution.py:270
  145.5 4.1 %bitcast_convert_fusion = f32[1024,1024]{1,0:T(8,128)} fusion(bf16[2,512,1024]{2,1,0:T(8,128)(2,1)} %shard_map.17), kind=kLoop, calls=%fused_computation.4 | loop fusion | flops 1048576 | bytes 6291456 | tf_op jit(solution)/shard_map/convert_element_type | solution.py:284
  (4 shorter events, 0.1 us)
Async XLA Ops:
  8.9 1.6 %collective-permute-start = (f32[3,1024]{1,0:T(4,128)S(1)}, f32[3,1024]{1,0:T(4,128)S(1)}, u32[]{:S(2)}, u32[]{:S(2)}) collective-permute-start(f32[3,1024]{1,0:T(4,128)S(1)} %pad_maximum_fusion.1), channel_id=1, source_target_pairs={{0,8},{8,0},{16,24},{24,16},{1,9},{9,1},{17,25},{25,17},{2,10},{10... | collective-permute-start | bytes 36872 | tf_op jit(solution)/shard_map/ppermute | solution.py:16
  10.5 2.7 %collective-permute-start.1 = (f32[3,1024]{1,0:T(4,128)S(1)}, f32[3,1024]{1,0:T(4,128)S(1)}, u32[]{:S(2)}, u32[]{:S(2)}) collective-permute-start(f32[3,1024]{1,0:T(4,128)S(1)} %fusion.2), channel_id=1, source_target_pairs={{0,16},{8,24},{16,0},{24,8},{1,17},{9,25},{17,1},{25,9},{2,18},{10... | collective-permute-start | bytes 36872 | tf_op jit(solution)/shard_map/ppermute | solution.py:16
